TPU v7x, 32 devices: a whole 2x2x4 slice. The times are simulated.
32 devices in a mesh: row: 8 (over z, x), col: 4 (over y, core).
Axes of the slice: x: 2, y: 2, z: 4, core: 2. Of those that a mesh axis runs over, the one named last changes fastest.
Arguments:
- panel_block: float32 [20480, 512], P('row', 'col'), may hold values from -12 to 12
- trailing: float32 [20480, 20480], P('row', 'col'), may hold values from -6 to 6
Outputs:
- updated: float32 [20480, 20480], P('row', 'col')
All inputs are finite; a program needn't handle non-finite values.
Results may differ from a plain program's by a relative error of at most 0.0003.
Values sent between devices are 32-bit elements; how exact they have to be, the bound alone decides.
No kernel may reach another device: no remote copies, remote signals or barrier semaphores. Data moves between devices by JAX's collectives and lax.ppermute only.
A program may use at most 192 MiB of HBM per device.

v0:
```python
import jax
import jax.numpy as jnp
from jax import lax
from jax.sharding import PartitionSpec as P

N = 20480


def on_device(panel_block, trailing):
    local_rows = panel_block.shape[0]
    local_width = panel_block.shape[1]
    rows_count = lax.axis_size("row")
    cols_count = lax.axis_size("col")
    copies = rows_count // cols_count
    row_owner = lax.axis_index("row")
    col_owner = lax.axis_index("col")
    mc_rows = lax.all_gather(panel_block, "col", axis=1, tiled=True)
    squares = lax.psum(jnp.sum(mc_rows * mc_rows), "row")
    column_block = lax.all_gather(panel_block, "row", axis=0, tiled=True)
    shaped = column_block.reshape(copies, cols_count, local_rows, local_width)
    moved = lax.all_to_all(shaped, "col", split_axis=1, concat_axis=3, tiled=True)
    stacked = moved.reshape(copies, local_rows, mc_rows.shape[1])
    mr_rows = jnp.transpose(stacked, (1, 0, 2)).reshape(copies * local_rows, stacked.shape[2])
    update = lax.dot_general(
        mc_rows,
        mr_rows,
        (((1,), (1,)), ((), ())),
        precision=lax.Precision.HIGHEST,
        preferred_element_type=jnp.float32,
    )
    row_index = jnp.arange(local_rows, dtype=jnp.int32) * rows_count + row_owner
    col_index = jnp.arange(mr_rows.shape[0], dtype=jnp.int32) * cols_count + col_owner
    lower_part = row_index[:, None] >= col_index[None, :]
    factor = 0.8 * jnp.sqrt(jnp.float32(N)) / jnp.sqrt(squares + 1e-06)
    return trailing - factor * jnp.where(lower_part, update, jnp.zeros_like(update))


def solution(mesh):
    in_specs = (P("row", "col"), P("row", "col"))
    out_specs = P("row", "col")
    return jax.shard_map(
        on_device, mesh=mesh, in_specs=in_specs, out_specs=out_specs, check_vma=False
    )
```

profile of v0, /device:TPU:0, one launch (start us, length us, event | category | flops | bytes accessed | tf_op | source)
XLA Modules:
  0.0 456.7 jit_solution(3020572873124051038)
XLA Ops:
  6.5 0.0 all-gather.5.cloned.1.call-start
  6.5 0.7 all-gather.5.cloned.1.call-update
  7.3 0.0 all-gather.3.cloned.1.call-start
  7.3 0.7 all-gather.3.cloned.1.call-update
  8.0 154.8 %all-gather.5.cloned.1.call-done = f32[20480,128]{1,0:T(8,128)} async-done(((f32[2560,128]{1,0:T(8,128)}), f32[20480,128]{1,0:T(8,128)}) %all-gather.5.cloned.1.call-update) | async-done | bytes 10485776 | tf_op jit(solution)/shard_map/all_gather | solution.py:19
  162.8 9.6 %copy.6 = f32[2,4,2560,128]{3,2,0,1:T(8,128)} copy(f32[2,4,2560,128]{3,2,1,0:T(8,128)} %bitcast.11) | data formatting | bytes 20971520 | tf_op jit(solution)/shard_map/reshape | solution.py:20
  172.4 6.0 %all-to-all-start = ((f32[2,4,2560,128]{3,2,0,1:T(8,128)}), f32[2,4,2560,128]{3,2,0,1:T(8,128)}, u32[]{:S(2)}, u32[]{:S(2)}) async-start(f32[2,4,2560,128]{3,2,0,1:T(8,128)} %copy.6), calls=%async_computation | async-start | bytes 20971520 | tf_op jit(solution)/shard_map/all_to_all | solution.py:21
  178.5 45.0 %all-gather.3.cloned.1.call-done = f32[2560,512]{1,0:T(8,128)} async-done(((f32[2560,128]{1,0:T(8,128)}), f32[2560,512]{1,0:T(8,128)}) %all-gather.3.cloned.1.call-update) | async-done | bytes 5242896 | tf_op jit(solution)/shard_map/all_gather | solution.py:17
  223.4 4.5 multiply_reduce_fusion
  227.9 25.2 %psum.7 = f32[]{:T(128)} all-reduce(f32[]{:T(128)} %multiply_reduce_fusion), channel_id=1, replica_groups=mesh['row'=8,'col'=4] {'row'}, use_global_device_ids=true, to_apply=%region_1.0 | all-reduce | flops 1 | bytes 8 | tf_op jit(solution)/shard_map/psum | solution.py:18
  253.8 60.0 %all-to-all-done = f32[2,4,2560,128]{3,2,0,1:T(8,128)} async-done(((f32[2,4,2560,128]{3,2,0,1:T(8,128)}), f32[2,4,2560,128]{3,2,0,1:T(8,128)}, u32[]{:S(2)}, u32[]{:S(2)}) %all-to-all-start) | async-done | bytes 10485792 | tf_op jit(solution)/shard_map/all_to_all | solution.py:21
  313.8 11.4 %copy.7 = f32[2,4,2560,128]{2,3,1,0:T(8,128)} copy(f32[2,4,2560,128]{3,2,0,1:T(8,128)} %all-to-all-done) | data formatting | bytes 20971520 | tf_op jit(solution)/shard_map/all_to_all | solution.py:21
  325.2 16.1 %copy.8 = f32[2560,2,512]{2,1,0:T(2,128)} copy(f32[2560,2,512]{0,2,1:T(8,128)} %bitcast.10) | data formatting | bytes 20971520 | tf_op jit(solution)/shard_map/transpose | solution.py:23
  341.3 13.3 %reshape.22 = f32[5120,512]{1,0:T(8,128)} reshape(f32[2560,2,512]{2,1,0:T(2,128)} %copy.8) | data formatting | bytes 20971520 | tf_op jit(solution)/shard_map/reshape | solution.py:23
  354.5 95.4 %multiply_subtract_fusion = f32[2560,5120]{1,0:T(8,128)} fusion(f32[2560,5120]{1,0:T(8,128)} %param.3, f32[2560,512]{1,0:T(8,128)} %all-gather.3.cloned.1.call-done, f32[5120,512]{1,0:T(8,128)} %reshape.22, s32[5120]{0:T(1024)S(1)} %multiply_add_fusion, f32[]{:T(128)S(6)} %div.3, s32[2560]{0:T(1024)S(1)} %multiply_add_fusion.1), kind=kOutput, calls=%fused_computation | convolution fusion | flops 80583065600 | bytes 120616960 | tf_op jit(solution)/shard_map/dot_general | solution.py:24
  (2 shorter events, 0.0 us)
Async XLA Ops:
  6.5 156.2 %all-gather.5.cloned.1.call-start = ((), (), s32[]{:S(2)}) async-start(), calls=%async_computation.2 | async-start | bytes 11796480 | tf_op jit(solution)/shard_map/all_gather | solution.py:19
  7.3 216.2 %all-gather.3.cloned.1.call-start = ((), (), s32[]{:S(2)}) async-start(), calls=%async_computation.1 | async-start | bytes 6553600 | tf_op jit(solution)/shard_map/all_gather | solution.py:17
  172.4 141.4 %all-to-all-start = ((f32[2,4,2560,128]{3,2,0,1:T(8,128)}), f32[2,4,2560,128]{3,2,0,1:T(8,128)}, u32[]{:S(2)}, u32[]{:S(2)}) async-start(f32[2,4,2560,128]{3,2,0,1:T(8,128)} %copy.6), calls=%async_computation | async-start | bytes 20971520 | tf_op jit(solution)/shard_map/all_to_all | solution.py:21
Sparse Core Ops, SparseCore 0:
  9.5 153.2 all-gather.4
  164.3 59.0 all-gather.2
where the time goes:
time: 458 us; the launch traced here: 457 us
  waiting for transfers between devices  261 us (57%)
  matrix products  95.4 us (21%)
  local copies, waits for them, and re-layouts  50.4 us (11%)
  blocking collectives  25.2 us (6%)
  between operations  14.1 us (3%)
  starting transfers between devices  6.08 us (1%)
    all_gather x1, waiting for transfers between devices, on_device(): column_block = lax.all_gather(panel_block, 'row', axis=0, tiled=True)  155 us
    dot_general x1, matrix products, on_device(): lax.dot_general(mc_rows, mr_rows, (((1,), (1,)), ((), ())), precision=lax...  95.4 us
    all_to_all x1, waiting for transfers between devices, on_device(): lax.all_to_all(shaped, 'col', split_axis=1, concat_axis=3, tiled=True)  60 us
    all_gather x1, waiting for transfers between devices, on_device(): mc_rows = lax.all_gather(panel_block, 'col', axis=1, tiled=True)  45 us
    psum x1, blocking collectives, on_device(): squares = lax.psum(jnp.sum(mc_rows * mc_rows), 'row')  25.2 us
    transpose x1, local copies, waits for them, and re-layouts, on_device(): jnp.transpose(stacked, (1, 0, 2))  16.1 us
    reshape x1, local copies, waits for them, and re-layouts, on_device(): jnp.transpose(stacked, (1, 0, 2))  13.3 us
    all_to_all x1, local copies, waits for them, and re-layouts, on_device(): lax.all_to_all(shaped, 'col', split_axis=1, concat_axis=3, tiled=True)  11.4 us
  transfers between devices with their start and end apart: 3, of which 3 were waited for; matrix products, arithmetic and copies ran while one was open for 3% of the time, Pallas kernels for 0%

commit v1 on v0

--- a/solution.py
+++ b/solution.py
@@ -18,7 +18,10 @@
     squares = lax.psum(jnp.sum(mc_rows * mc_rows), "row")
     column_block = lax.all_gather(panel_block, "row", axis=0, tiled=True)
     shaped = column_block.reshape(copies, cols_count, local_rows, local_width)
-    moved = lax.all_to_all(shaped, "col", split_axis=1, concat_axis=3, tiled=True)
+    moved = jnp.concatenate(
+        lax.all_to_all(jnp.stack(jnp.split(shaped, lax.axis_size("col"), axis=1)), "col", 0, 0),
+        axis=3,
+    )
     stacked = moved.reshape(copies, local_rows, mc_rows.shape[1])
     mr_rows = jnp.transpose(stacked, (1, 0, 2)).reshape(copies * local_rows, stacked.shape[2])
     update = lax.dot_general(

time: 458 us -> 511 us (1.12)
  local copies, waits for them, and re-layouts: 50.4 us -> 150 us
  waiting for transfers between devices: 261 us -> 209 us
    sub x0 -> x1, local copies, waits for them, and re-layouts: none -> 52 us  [on_device(): trailing - factor * jnp.where(lower_part, update, jnp.zeros_like(update))]
    unnamed x0 -> x1, local copies, waits for them, and re-layouts: none -> 52 us
    all_to_all x1, waiting for transfers between devices: 60 us -> 8.12 us  [on_device(): lax.all_to_all(jnp.stack(jnp.split(shaped, lax.axis_size('col'), axis=1))...]
    all_to_all x1 -> x0, local copies, waits for them, and re-layouts: 11.4 us -> none  [on_device(): lax.all_to_all(shaped, 'col', split_axis=1, concat_axis=3, tiled=True)]
  transfers between devices with their start and end apart: 3 -> 3, of which waited for: 3 -> 3; matrix products, arithmetic and copies ran while one was open for 3% -> 13% of each run, Pallas kernels for 0% -> 0%
where the time goes in v1:
time: 511 us; the launch traced here: 509 us
  waiting for transfers between devices  209 us (41%)
  local copies, waits for them, and re-layouts  150 us (29%)
  matrix products  95.3 us (19%)
  blocking collectives  25.1 us (5%)
  between operations  14.2 us (3%)
  other arithmetic  9.47 us (2%)
  starting transfers between devices  6.08 us (1%)
    all_gather x1, waiting for transfers between devices, on_device(): column_block = lax.all_gather(panel_block, 'row', axis=0, tiled=True)  155 us
    dot_general x1, matrix products, on_device(): lax.dot_general(mc_rows, mr_rows, (((1,), (1,)), ((), ())), precision=lax...  95.3 us
    sub x1, local copies, waits for them, and re-layouts, on_device(): trailing - factor * jnp.where(lower_part, update, jnp.zeros_like(update))  52 us
    unnamed x1, local copies, waits for them, and re-layouts  52 us
    all_gather x1, waiting for transfers between devices, on_device(): mc_rows = lax.all_gather(panel_block, 'col', axis=1, tiled=True)  44.6 us
    psum x1, blocking collectives, on_device(): squares = lax.psum(jnp.sum(mc_rows * mc_rows), 'row')  25.1 us
    transpose x1, local copies, waits for them, and re-layouts, on_device(): jnp.transpose(stacked, (1, 0, 2))  16.1 us
    reshape x1, local copies, waits for them, and re-layouts, on_device(): jnp.transpose(stacked, (1, 0, 2))  13.3 us
  transfers between devices with their start and end apart: 3, of which 3 were waited for; matrix products, arithmetic and copies ran while one was open for 13% of the time, Pallas kernels for 0%

profile of v1, /device:TPU:0, one launch (start us, length us, event | category | flops | bytes accessed | tf_op | source)
XLA Modules:
  0.0 508.8 jit_solution(515382029829197417)
XLA Ops:
  6.5 0.0 all-gather.5.cloned.1.call-start
  6.5 0.7 all-gather.5.cloned.1.call-update
  7.3 0.0 all-gather.3.cloned.1.call-start
  7.3 0.7 all-gather.3.cloned.1.call-update
  8.0 154.8 %all-gather.5.cloned.1.call-done = f32[20480,128]{1,0:T(8,128)} async-done(((f32[2560,128]{1,0:T(8,128)}), f32[20480,128]{1,0:T(8,128)}) %all-gather.5.cloned.1.call-update) | async-done | bytes 10485776 | tf_op jit(solution)/shard_map/all_gather | solution.py:19
  162.8 4.8 slice_bitcast_fusion.3
  167.6 4.9 pad_maximum_fusion
  172.6 6.0 %all-to-all-start = ((f32[4,2,1,2560,128]{4,3,1,2,0:T(8,128)}), f32[4,2,1,2560,128]{4,3,1,2,0:T(8,128)}, u32[]{:S(2)}, u32[]{:S(2)}) async-start(f32[4,2,1,2560,128]{4,3,1,2,0:T(8,128)} %pad_maximum_fusion), calls=%async_computation | async-start | bytes 20971520 | tf_op jit(solution)/shard_map/all_to_all | solution.py:22
  178.6 44.6 %all-gather.3.cloned.1.call-done = f32[2560,512]{1,0:T(8,128)} async-done(((f32[2560,128]{1,0:T(8,128)}), f32[2560,512]{1,0:T(8,128)}) %all-gather.3.cloned.1.call-update) | async-done | bytes 5242896 | tf_op jit(solution)/shard_map/all_gather | solution.py:17
  223.2 4.5 multiply_reduce_fusion
  227.8 52.0 %copy.19 = f32[2560,5120]{0,1:T(8,128)} copy(f32[2560,5120]{1,0:T(8,128)} %param.3) | data formatting | bytes 104857600 | tf_op args[1]
  279.8 25.1 %psum.7 = f32[]{:T(128)} all-reduce(f32[]{:T(128)} %multiply_reduce_fusion), channel_id=1, replica_groups=mesh['row'=8,'col'=4] {'row'}, use_global_device_ids=true, to_apply=%region_1.0 | all-reduce | flops 1 | bytes 8 | tf_op jit(solution)/shard_map/psum | solution.py:18
  305.6 8.1 %all-to-all-done = f32[4,2,1,2560,128]{4,3,1,2,0:T(8,128)} async-done(((f32[4,2,1,2560,128]{4,3,1,2,0:T(8,128)}), f32[4,2,1,2560,128]{4,3,1,2,0:T(8,128)}, u32[]{:S(2)}, u32[]{:S(2)}) %all-to-all-start) | async-done | bytes 10485792 | tf_op jit(solution)/shard_map/all_to_all | solution.py:22
  313.8 11.5 %copy.17 = f32[2,1,2560,4,128]{2,4,3,0,1:T(8,128)} copy(f32[2,1,2560,4,128]{4,2,0,1,3:T(8,128)} %bitcast.5) | data formatting | bytes 20971520 | tf_op jit(solution)/shard_map/reshape | solution.py:21
  325.3 16.1 %copy.18 = f32[2560,2,512]{2,1,0:T(2,128)} copy(f32[2560,2,512]{0,2,1:T(8,128)} %bitcast.27) | data formatting | bytes 20971520 | tf_op jit(solution)/shard_map/transpose | solution.py:26
  341.4 13.3 %reshape.21 = f32[5120,512]{1,0:T(8,128)} reshape(f32[2560,2,512]{2,1,0:T(2,128)} %copy.18) | data formatting | bytes 20971520 | tf_op jit(solution)/shard_map/reshape | solution.py:26
  354.6 95.3 %fusion.1 = f32[2560,5120]{0,1:T(8,128)} fusion(f32[2560,5120]{0,1:T(8,128)} %copy.19, f32[5120,512]{1,0:T(8,128)} %reshape.21, f32[2560,512]{1,0:T(8,128)} %all-gather.3.cloned.1.call-done, s32[2560]{0:T(1024)S(1)} %multiply_add_fusion.1, f32[]{:T(128)S(6)} %div.3, s32[5120]{0:T(1024)S(1)} %multiply_add_fusion), kind=kOutput, calls=%fused_computation.2 | convolution fusion | flops 80583065600 | bytes 120616960 | tf_op jit(solution)/shard_map/dot_general | solution.py:27
  449.9 52.0 %copy.20 = f32[2560,5120]{1,0:T(8,128)} copy(f32[2560,5120]{0,1:T(8,128)} %fusion.1) | data formatting | bytes 104857600 | tf_op jit(solution)/shard_map/sub | solution.py:38
  (2 shorter events, 0.0 us)
Async XLA Ops:
  6.5 156.2 %all-gather.5.cloned.1.call-start = ((), (), s32[]{:S(2)}) async-start(), calls=%async_computation.2 | async-start | bytes 11796480 | tf_op jit(solution)/shard_map/all_gather | solution.py:19
  7.3 216.0 %all-gather.3.cloned.1.call-start = ((), (), s32[]{:S(2)}) async-start(), calls=%async_computation.1 | async-start | bytes 6553600 | tf_op jit(solution)/shard_map/all_gather | solution.py:17
  172.6 141.2 %all-to-all-start = ((f32[4,2,1,2560,128]{4,3,1,2,0:T(8,128)}), f32[4,2,1,2560,128]{4,3,1,2,0:T(8,128)}, u32[]{:S(2)}, u32[]{:S(2)}) async-start(f32[4,2,1,2560,128]{4,3,1,2,0:T(8,128)} %pad_maximum_fusion), calls=%async_computation | async-start | bytes 20971520 | tf_op jit(solution)/shard_map/all_to_all | solution.py:22
Sparse Core Ops, SparseCore 0:
  9.5 153.2 all-gather.4
  164.3 58.8 all-gather.2
